TPU v7x, 32 devices: a whole 2x2x4 slice. The times are simulated.
32 devices in a mesh: dp: 8 (over y, x, core), tensor: 4 (over z).
Axes of the slice: x: 2, y: 2, z: 4, core: 2. Of those that a mesh axis runs over, the one named last changes fastest.
Arguments:
- rollout: bfloat16 [2048, 6144], P('dp', 'tensor'), may hold values from -100 to 100
- lengths: int32 [8, 32], replicated, may hold values from 1 to 8, as said below
- packing: int32 [256], replicated, may hold values from 0 to 255, as said below
- norm_gain: float32 [6144], replicated, may hold values from 0.5 to 4
- query_weight: bfloat16 [6144, 1024], P(None, 'tensor'), may hold values from -0.078125 to 0.078125
- keyval_weight: bfloat16 [6144, 256], P(None, 'tensor'), may hold values from -0.078125 to 0.078125
- out_weight: bfloat16 [1024, 6144], P('tensor'), may hold values from -0.1875 to 0.1875
Outputs:
- layer_out: bfloat16 [2048, 6144], P('dp', 'tensor')
Inputs may be any that keep to these rules, and one draw needn't show every extreme that they name: lengths[s, k] is the number of tokens of response k of source s; some response has 8 tokens in every draw. `packing`: a permutation of 0 .. 255; response r comes from source r // 32; every owner receives exactly 32 responses, exactly 4 of them from each source.
All inputs are finite; a program needn't handle non-finite values.
Results may differ from a plain program's by a relative error of at most 0.015.
Values may be sent and summed in bfloat16 or wider, within the bound.
A program may use at most 64 MiB of HBM per device.

v0:
```python
import functools
import math

import numpy as np
import jax
import jax.numpy as jnp
from jax import lax
from jax.experimental import pallas as pl
from jax.experimental.pallas import tpu as pltpu
from jax.sharding import PartitionSpec as P

D = 6144
HD = 128
HQ_DEV = 2
GROUP = 8


epsilon = 1e-05
rope_base = 500000.0


def owner_map(lengths, packing, owner_id, pack_len):
    per_source = lengths.shape[1]
    chosen = lax.dynamic_slice_in_dim(packing, owner_id * per_source, per_source)
    ordered = jnp.take(lengths.reshape(-1), chosen)
    doc_start = jnp.cumsum(ordered) - ordered
    places = jnp.arange(pack_len, dtype=jnp.int32)
    inside = (places[:, None] >= doc_start[None, :]) & (
        places[:, None] < (doc_start + ordered)[None, :]
    )
    is_valid = jnp.any(inside, axis=1)
    slot_of = jnp.sum(
        jnp.where(inside, jnp.arange(per_source, dtype=jnp.int32)[None, :], 0), axis=1
    )
    response = jnp.take(chosen, slot_of)
    position = jnp.where(is_valid, places - jnp.take(doc_start, slot_of), 0)
    doc_id = jnp.where(is_valid, slot_of, per_source)
    return (response, position, doc_id, is_valid)


def rotate(values, position, head_dim):
    half_dim = head_dim // 2
    frequency = rope_base ** (-jnp.arange(half_dim, dtype=jnp.float32) * 2.0 / head_dim)
    angles = position.astype(jnp.float32)[:, None] * frequency[None, :]
    cosine = jnp.concatenate([jnp.cos(angles), jnp.cos(angles)], axis=1)[:, None, :]
    sine_table = jnp.concatenate([jnp.sin(angles), jnp.sin(angles)], axis=1)[:, None, :]
    turned = jnp.concatenate([-values[..., half_dim:], values[..., :half_dim]], axis=-1)
    return values * cosine + turned * sine_table


def plain_body(rollout, lengths, packing, norm_gain, query_weight, keyval_weight, out_weight):
    owner_id = lax.axis_index("dp")
    tensor_index = lax.axis_index("tensor")
    tensor_count = lax.axis_size("tensor")
    pack_len = rollout.shape[0]
    per_source = lengths.shape[1]
    response, position, doc_id, is_valid = owner_map(lengths, packing, owner_id, pack_len)
    source_start = jnp.cumsum(lengths, axis=1) - lengths
    global_row = (
        response // per_source * pack_len + jnp.take(source_start.reshape(-1), response) + position
    )
    portion = lax.all_gather(rollout, "dp", axis=0, tiled=True)
    within = is_valid & (global_row >= 0) & (global_row < portion.shape[0])
    picked = jnp.take(portion, jnp.clip(global_row, 0, portion.shape[0] - 1), axis=0)
    packed = jnp.where(within[:, None], picked, jnp.zeros_like(rollout))
    widened = lax.all_gather(packed, "tensor", axis=1, tiled=True).astype(jnp.float32)
    scaled = (widened * norm_gain[None, :]).astype(jnp.bfloat16)
    query_acc = jnp.dot(scaled, query_weight, preferred_element_type=jnp.float32)
    keyval_acc = jnp.dot(scaled, keyval_weight, preferred_element_type=jnp.float32)
    squares = jnp.sum(widened * widened, axis=1)
    query_acc, keyval_acc, squares = (query_acc, keyval_acc, squares)
    inverse = lax.rsqrt(squares / D + epsilon)
    queries = query_acc * inverse[:, None]
    keyval_share = (keyval_acc * inverse[:, None]).astype(jnp.bfloat16)
    keyval_all = lax.all_gather(keyval_share, "tensor", axis=1, tiled=True)
    kv_count = keyval_weight.shape[1] * tensor_count // (2 * HD)
    shared_head = tensor_index * HQ_DEV // GROUP
    keys = lax.dynamic_slice_in_dim(keyval_all, shared_head * HD, HD, 1)
    values = lax.dynamic_slice_in_dim(keyval_all, (kv_count + shared_head) * HD, HD, 1)
    q_rot = rotate(queries.reshape(pack_len, HQ_DEV, HD), position, HD).astype(jnp.bfloat16)
    k_rot = rotate(keys.astype(jnp.float32)[:, None, :], position, HD)[:, 0, :].astype(jnp.bfloat16)
    scores = jnp.einsum(
        "qhd,kd->hqk", q_rot, k_rot, preferred_element_type=jnp.float32
    ) / math.sqrt(HD)
    places = jnp.arange(pack_len, dtype=jnp.int32)
    allowed = (doc_id[:, None] == doc_id[None, :]) & (places[None, :] <= places[:, None])
    masked = jnp.where(allowed[None], scores, -jnp.inf)
    row_max = jnp.max(masked, axis=2, keepdims=True)
    exponent = jnp.exp(masked - row_max)
    weights = (exponent / jnp.sum(exponent, axis=2, keepdims=True)).astype(jnp.bfloat16)
    context = jnp.einsum("hqk,kd->qhd", weights, values, preferred_element_type=jnp.float32)
    context = context.astype(jnp.bfloat16).reshape(pack_len, HQ_DEV * HD)
    partial_sum = jnp.dot(context, out_weight, preferred_element_type=jnp.float32)
    summed = lax.psum_scatter(
        partial_sum.astype(jnp.bfloat16), "tensor", scatter_dimension=1, tiled=True
    ).astype(jnp.float32)
    result = jnp.where(is_valid[:, None], summed + packed.astype(jnp.float32), 0.0)
    return result.astype(jnp.bfloat16)


MESH = pl.DeviceIdType.MESH
CORES = 2
HALO = 16


def aligned(index, size):
    return pl.multiple_of(index * size, size)


def fused_kernel(
    cfg, pk_hbm, len_hbm, gain_hbm, tab_hbm, roll_hbm, w_in, k_in, o_in, out,
    pk_buf, len_buf, gain, tab, wbuf, kbuf, obuf, roll_in, sendb, recvb, packed, scaled, q_part, kv_part, q_recv, kv_recv, ctx,
    pos_buf, valid_buf, acc, sq_part, sq_recv, send_sems, recv_sems, local_sems,
):
    n_dp, n_t, length, feat, per_source = cfg
    chips = n_dp // CORES
    w_sub = feat // n_dp
    kd = k_in.shape[0]
    k_rows, k_cols = kd // chips, feat // CORES
    o_rows = o_in.shape[0]
    o_sub = o_rows // n_dp
    block = length // n_dp
    most = length // per_source
    rows = length // n_t
    qd = w_in.shape[1]
    me = lax.axis_index("dp")
    t = lax.axis_index("tensor")
    core = lax.rem(me, CORES)
    chip = lax.div(me, CORES)
    partner = chip * CORES + (CORES - 1 - core)

    def t_at(k):
        return lax.rem(t + k, n_t)

    def chip_at(k):
        return lax.rem(chip + k, chips) * CORES + core

    small = [
        pltpu.make_async_copy(source, target, local_sems.at[4 + i])
        for i, (source, target) in enumerate(
            (
                (pk_hbm, pk_buf),
                (len_hbm, len_buf),
                (gain_hbm.at[:, pl.ds(aligned(t, feat), feat)], gain),
                (tab_hbm, tab),
            )
        )
    ]
    load = pltpu.make_async_copy(roll_hbm, roll_in, local_sems.at[2])
    for copy in [*small, load]:
        copy.start()

    barrier = pltpu.get_barrier_semaphore()
    for k in range(1, n_dp):
        pl.semaphore_signal(
            barrier, inc=1, device_id=(lax.rem(me + k, n_dp), t), device_id_type=MESH
        )
    for k in range(1, n_t):
        pl.semaphore_signal(barrier, inc=1, device_id=(me, t_at(k)), device_id_type=MESH)
    pl.semaphore_wait(barrier, n_dp + n_t - 2)

    started = []

    def send(source, target, device):
        at = len(started)
        copy = pltpu.make_async_remote_copy(
            src_ref=source,
            dst_ref=target,
            send_sem=send_sems.at[at],
            recv_sem=recv_sems.at[at],
            device_id=device,
            device_id_type=MESH,
        )
        copy.start()
        started.append(copy)
        return copy

    def w_at(u, h, c):
        return wbuf.at[u, pl.ds(aligned(h * CORES + c, w_sub), w_sub)]

    def k_at(u, h, c):
        return kbuf.at[
            pl.ds(aligned(u * chips + h, k_rows), k_rows), pl.ds(aligned(c, k_cols), k_cols)
        ]

    def o_at(u, h, c):
        return obuf.at[u, pl.ds(aligned(h * CORES + c, o_sub), o_sub)]

    w_first, k_first, o_first = {}, {}, {}
    for k in range(1, n_t):
        to = t_at(k)
        k_first[k] = send(
            k_in.at[
                pl.ds(aligned(chip, k_rows), k_rows),
                pl.ds(aligned(to * CORES + core, k_cols), k_cols),
            ],
            k_at(t, chip, core),
            (me, to),
        )
    for k in range(1, n_t):
        to = t_at(k)
        w_first[k] = send(
            w_in.at[pl.ds(aligned(to * n_dp + me, w_sub), w_sub)], w_at(t, chip, core), (me, to)
        )
    own_w = pltpu.make_async_copy(
        w_in.at[pl.ds(aligned(t, feat), feat)], wbuf.at[t], local_sems.at[0]
    )
    own_w.start()
    own_k = pltpu.make_async_copy(
        k_in.at[:, pl.ds(aligned(t, feat), feat)],
        kbuf.at[pl.ds(aligned(t, kd), kd)],
        local_sems.at[3],
    )
    own_k.start()
    for k in range(1, n_t):
        to = t_at(k)
        o_first[k] = send(
            o_in.at[pl.ds(aligned(me, o_sub), o_sub), pl.ds(aligned(to, feat), feat)],
            o_at(t, chip, core),
            (me, to),
        )
    own_o = pltpu.make_async_copy(
        o_in.at[:, pl.ds(aligned(t, feat), feat)], obuf.at[t], local_sems.at[1]
    )
    own_o.start()

    down = lax.broadcasted_iota(jnp.int32, (length, length), 0).astype(jnp.float32)
    across = lax.broadcasted_iota(jnp.int32, (length, length), 1).astype(jnp.float32)

    def part(value, size):
        return jnp.floor((value + 0.5) * (1.0 / size))

    def pick(mask, value, axis):
        return jnp.sum(jnp.where(mask, value, 0.0), axis=axis, keepdims=True)

    same = part(down, per_source) == part(across, per_source)
    diagonal = down == across
    for copy in small:
        copy.wait()
    len_all = len_buf[...].astype(jnp.float32)
    source_of = part(down[:, :1], per_source)
    table = jnp.zeros((length, per_source), jnp.float32)
    for i in range(n_dp):
        table = jnp.where(source_of == float(i), len_all[i : i + 1, :], table)
    within = down[:, :per_source] - source_of * per_source
    len_c = pick(across[:, :per_source] == within, table, 1)
    len_r = pick(diagonal, len_c, 0)
    pk_r = pk_buf[...].astype(jnp.float32)
    pk_c = pick(diagonal, pk_r, 1)
    src_start = pick(same & (across < down), len_r, 1)
    chosen = down == pk_r
    q_len_r = pick(chosen, len_c, 0)
    q_start_r = pick(chosen, src_start, 0)
    q_len_c = pick(across == pk_c, len_r, 1)
    earlier = same & (down < across)
    doc_start_r = pick(earlier, q_len_c, 0)
    q_src_r = part(pk_r, per_source)
    slot_r = pick(earlier & (part(pk_c, per_source) == q_src_r), 1.0, 0)
    mine = me.astype(jnp.float32)
    across_1 = across[:1]
    down_1 = down[:, :1]
    owner_r = part(across_1, per_source)
    target = jnp.where(q_src_r == mine, owner_r * (per_source // n_dp) + slot_r, -1.0)
    group = part(down_1, most)
    match = target == group
    token = down_1 - group * most
    row_sent = jnp.where(token < pick(match, q_len_r, 1), pick(match, q_start_r, 1) + token, -1.0)
    take_send = (across == row_sent).astype(jnp.float32).astype(jnp.bfloat16)
    inside = (owner_r == mine) & (doc_start_r <= down) & (down < doc_start_r + q_len_r)
    is_valid = pick(inside, 1.0, 1)
    position = (down_1 - pick(inside, doc_start_r, 1)) * is_valid
    row_got = jnp.where(
        is_valid > 0.0, pick(inside, q_src_r * block + slot_r * most, 1) + position, -1.0
    )
    take_recv = (across == row_got).astype(jnp.float32).astype(jnp.bfloat16)
    pos_buf[:HALO, :] = jnp.zeros((HALO, HD), jnp.float32)
    pos_buf[HALO:, :] = jnp.broadcast_to(position, (length, HD))
    valid_buf[...] = jnp.broadcast_to(is_valid, (length, HD))

    tile = 256
    tiles = feat // tile

    def send_tile(i, carry):
        at = pl.ds(aligned(i, tile), tile)
        sendb[:, at] = jnp.dot(
            take_send, roll_in[:, at], preferred_element_type=jnp.float32
        ).astype(jnp.bfloat16)
        return carry

    load.wait()
    lax.fori_loop(0, tiles, send_tile, 0)

    rows_of = {}
    for k in range(1, n_dp):
        to = lax.rem(me + k, n_dp)
        rows_of[k] = send(
            sendb.at[pl.ds(aligned(to, block), block)],
            recvb.at[pl.ds(aligned(me, block), block)],
            (to, t),
        )
    keep = pl.ds(aligned(me, block), block)
    recvb[keep, :] = sendb[keep, :]

    def spread(at, first, j):
        first[j].wait_recv()
        ref = at(t_at(n_t - j), chip, core)
        return [send(ref, ref, (chip_at(k), t)) for k in range(1, chips)]

    def share(at, hops, j):
        last = []
        for k in range(chips):
            if k:
                hops[k - 1].wait_recv()
            ref = at(t_at(n_t - j), lax.rem(chip + chips - k, chips), core)
            last.append(send(ref, ref, (partner, t)))
        return last

    others = range(1, n_t)
    k_hops = {j: spread(k_at, k_first, j) for j in others}
    w_hops = {1: spread(w_at, w_first, 1)}

    for k in range(1, n_dp):
        rows_of[k].wait_recv()

    def pack_tile(i, total):
        at = pl.ds(aligned(i, tile), tile)
        x = jnp.dot(take_recv, recvb[:, at], preferred_element_type=jnp.float32)
        packed[:, at] = x.astype(jnp.bfloat16)
        g = gain[:, at]
        scaled[:, at] = (x * g).astype(jnp.bfloat16)
        return total + jnp.sum(x * x, axis=1, keepdims=True)

    squares = lax.fori_loop(0, tiles, pack_tile, jnp.zeros((length, 1), jnp.float32))
    kv_part[:HALO, :] = jnp.zeros((HALO, 2 * HD), jnp.bfloat16)
    sq_part[...] = jnp.broadcast_to(pick(diagonal, squares, 0), (8, length))
    shares = []

    def reduce_rows(part_ref, recv_ref, extra, cols):
        for k in others:
            to = t_at(k)
            shares.append(
                send(
                    part_ref.at[pl.ds(aligned(to, rows), rows + extra), cols],
                    recv_ref.at[k - 1, :, cols],
                    (me, to),
                )
            )

    def project(j):
        u = t_at(n_t - j)
        cols = pl.ds(aligned(u, qd), qd)
        q_part[:, cols] = jnp.dot(
            scaled[...], wbuf[u], preferred_element_type=jnp.float32
        ).astype(jnp.bfloat16)
        reduce_rows(q_part, q_recv, 0, cols)

    own_w.wait()
    own_k.wait()
    for k in others:
        shares.append(send(sq_part, sq_recv.at[k - 1], (me, t_at(k))))
    project(n_t)
    for j in others[1:]:
        w_hops[j] = spread(w_at, w_first, j)
    k_last = [copy for j in others for copy in share(k_at, k_hops[j], j)]
    for copy in k_last:
        copy.wait_recv()
    kv_part[HALO:, : 2 * HD] = lax.dot_general(
        scaled[...], kbuf[...], (((1,), (1,)), ((), ())), preferred_element_type=jnp.float32
    ).astype(jnp.bfloat16)
    reduce_rows(kv_part, kv_recv, HALO, pl.ds(0, 2 * HD))
    w_last = share(w_at, w_hops[1], 1)
    o_hops = {}
    for j in others:
        if j + 1 in w_hops:
            following = share(w_at, w_hops[j + 1], j + 1)
        for copy in w_last:
            copy.wait_recv()
        w_last = following
        project(j)
        o_hops[j] = spread(o_at, o_first, j)
    for copy in shares:
        copy.wait_recv()

    keys_at = pl.ds(aligned(t, rows), rows + HALO)
    queries_at = pl.ds(aligned(t, rows), rows)
    kv = kv_part[keys_at, :].astype(jnp.float32)
    for k in range(n_t - 1):
        kv += kv_recv[k].astype(jnp.float32)
    sq = sq_part[:1, :]
    for k in range(n_t - 1):
        sq += sq_recv[k, :1, :]
    row_at = lax.broadcasted_iota(jnp.int32, (rows + HALO, length), 0) + (t * rows - HALO)
    sums = pick(lax.broadcasted_iota(jnp.int32, (rows + HALO, length), 1) == row_at, sq, 1)
    inverse = lax.rsqrt(sums / (feat * n_t) + epsilon)
    kv_bf = (kv[:, : 2 * HD] * inverse).astype(jnp.bfloat16)
    values = kv_bf[:, HD:]
    pos = pos_buf[keys_at, :]
    cosine = jnp.zeros((rows + HALO, HD), jnp.float32)
    sine = jnp.zeros((rows + HALO, HD), jnp.float32)
    for m in range(most):
        at_m = pos == float(m)
        cosine = jnp.where(at_m, tab[m : m + 1, :], cosine)
        sine = jnp.where(at_m, tab[most + m : most + m + 1, :], sine)

    def turn(v, c, s):
        return v * c + pltpu.roll(v, HD // 2, 1) * s

    k_rot = turn(kv_bf[:, :HD].astype(jnp.float32), cosine, sine).astype(jnp.bfloat16)
    q_down = lax.broadcasted_iota(jnp.int32, (rows, rows + HALO), 0).astype(jnp.float32)
    k_across = lax.broadcasted_iota(jnp.int32, (rows, rows + HALO), 1).astype(jnp.float32) - HALO
    allowed = (k_across <= q_down) & (k_across >= q_down - pos[HALO:, :1])
    gathers = []
    heads = q_part.shape[1] // HD
    for h in range(heads):
        cols = slice(h * HD, (h + 1) * HD)
        q = q_part[queries_at, cols].astype(jnp.float32)
        for k in range(n_t - 1):
            q += q_recv[k, :, cols].astype(jnp.float32)
        q_rot = turn(q * inverse[HALO:], cosine[HALO:], sine[HALO:]).astype(jnp.bfloat16)
        scores = lax.dot_general(
            q_rot, k_rot, (((1,), (1,)), ((), ())), preferred_element_type=jnp.float32
        ) * (1.0 / math.sqrt(HD))
        scores = jnp.where(allowed, scores, -jnp.inf)
        exponent = jnp.exp(scores - jnp.max(scores, axis=1, keepdims=True))
        weights = (exponent / jnp.sum(exponent, axis=1, keepdims=True)).astype(jnp.bfloat16)
        ctx[queries_at, cols] = jnp.dot(
            weights, values, preferred_element_type=jnp.float32
        ).astype(jnp.bfloat16)
        if (h + 1) % (heads // n_t) == 0:
            at = ctx.at[queries_at, pl.ds((h + 1 - heads // n_t) * HD, heads // n_t * HD)]
            for k in others:
                gathers.append(send(at, at, (me, t_at(k))))

    o_last = [copy for j in others for copy in share(o_at, o_hops[j], j)]
    own_o.wait()
    for copy in o_last:
        copy.wait_recv()

    for u in range(n_t):
        for copy in gathers[u * (n_t - 1) : (u + 1) * (n_t - 1)]:
            copy.wait_recv()

        def out_tile(i, carry, u=u):
            at = pl.ds(aligned(i, tile), tile)
            total = packed[:, at].astype(jnp.float32) if u == 0 else acc[:, at]
            total += jnp.dot(
                ctx[:, u * o_rows : (u + 1) * o_rows],
                obuf[u, :, at],
                preferred_element_type=jnp.float32,
            )
            if u < n_t - 1:
                acc[:, at] = total
            else:
                out[:, at] = jnp.where(valid_buf[:, :1] > 0.0, total, 0.0).astype(jnp.bfloat16)
            return carry

        lax.fori_loop(0, tiles, out_tile, 0)
    for copy in started:
        copy.wait_send()


def fused_body(rollout, lengths, packing, norm_gain, query_weight, keyval_weight, out_weight):
    n_dp, n_t = lax.axis_size("dp"), lax.axis_size("tensor")
    length, feat = rollout.shape
    per_source = lengths.shape[1]
    most = length // per_source
    qd, kd = query_weight.shape[1], keyval_weight.shape[1]
    frequency = np.float32(rope_base) ** (-np.arange(HD // 2, dtype=np.float32) * 2.0 / HD)
    angles = np.arange(most, dtype=np.float32)[:, None] * frequency[None, :].astype(np.float32)
    cos_tab = np.concatenate([np.cos(angles)] * 2, axis=1).astype(np.float32)
    sin_tab = np.concatenate([-np.sin(angles), np.sin(angles)], axis=1).astype(np.float32)
    rows = length // n_t
    chips = n_dp // CORES
    copies = 3 * (n_t - 1) * (1 + chips - 1 + chips) + (n_dp - 1) + (2 + 2 * n_t) * (n_t - 1)
    vmem = pl.BlockSpec(memory_space=pltpu.VMEM)
    hbm = pl.BlockSpec(memory_space=pl.ANY)
    bf, f32 = jnp.bfloat16, jnp.float32
    return pl.pallas_call(
        functools.partial(fused_kernel, (n_dp, n_t, length, feat, per_source)),
        out_shape=jax.ShapeDtypeStruct((length, feat), bf),
        in_specs=[hbm] * 8,
        out_specs=vmem,
        scratch_shapes=[
            pltpu.VMEM((1, packing.shape[0]), jnp.int32),
            pltpu.VMEM(lengths.shape, jnp.int32),
            pltpu.VMEM((1, feat), f32),
            pltpu.VMEM((2 * most, HD), f32),
            pltpu.VMEM((n_t, feat, qd), bf),
            pltpu.VMEM((n_t * kd, feat), bf),
            pltpu.VMEM((n_t, out_weight.shape[0], feat), bf),
            pltpu.VMEM((length, feat), bf),
            pltpu.VMEM((length, feat), bf),
            pltpu.VMEM((length, feat), bf),
            pltpu.VMEM((length, feat), bf),
            pltpu.VMEM((length, feat), bf),
            pltpu.VMEM((length, n_t * qd), bf),
            pltpu.VMEM((length + HALO, 2 * HD), bf),
            pltpu.VMEM((n_t - 1, rows, n_t * qd), bf),
            pltpu.VMEM((n_t - 1, rows + HALO, 2 * HD), bf),
            pltpu.VMEM((length, n_t * qd), bf),
            pltpu.VMEM((length + HALO, HD), f32),
            pltpu.VMEM((length, HD), f32),
            pltpu.VMEM((length, feat), f32),
            pltpu.VMEM((8, length), f32),
            pltpu.VMEM((n_t - 1, 8, length), f32),
            pltpu.SemaphoreType.DMA((copies,)),
            pltpu.SemaphoreType.DMA((copies,)),
            pltpu.SemaphoreType.DMA((8,)),
        ],
        compiler_params=pltpu.CompilerParams(
            collective_id=0, has_side_effects=True, vmem_limit_bytes=60 * 1024 * 1024
        ),
    )(
        packing[None, :], lengths, norm_gain[None, :],
        jnp.asarray(np.concatenate([cos_tab, sin_tab])), rollout, query_weight,
        keyval_weight.T, out_weight,
    )


def body(rollout, lengths, packing, norm_gain, query_weight, keyval_weight, out_weight):
    n_dp, n_t = lax.axis_size("dp"), lax.axis_size("tensor")
    length, feat = rollout.shape
    qd, kd = query_weight.shape[1], keyval_weight.shape[1]
    fits = (
        kd * n_t == 2 * HD
        and n_t == 4
        and kd % (HALO * n_dp // CORES) == 0
        and feat % (128 * CORES) == 0
        and n_dp % CORES == 0
        and length % (n_t * HALO) == 0
        and packing.shape[0] == length
        and (length // n_dp) % HALO == 0
        and feat % 512 == 0
        and lengths.shape[1] % n_dp == 0
    )
    chosen = fused_body if fits else plain_body
    return chosen(rollout, lengths, packing, norm_gain, query_weight, keyval_weight, out_weight)


def solution(mesh):
    in_specs = (
        P("dp", "tensor"),
        P(),
        P(),
        P(),
        P(None, "tensor"),
        P(None, "tensor"),
        P("tensor", None),
    )
    out_specs = P("dp", "tensor")
    return jax.shard_map(body, mesh=mesh, in_specs=in_specs, out_specs=out_specs, check_vma=False)
```

profile of v0, /device:TPU:0, one launch (start us, length us, event | category | flops | bytes accessed | tf_op | source)
XLA Modules:
  0.0 62.2 jit_solution(7939949982552157475)
XLA Ops:
  0.0 60.1 %shard_map.82 = bf16[256,1536]{1,0:T(8,128)(2,1)} custom-call(s32[1,256]{1,0:T(1,128)} %bitcast.5, s32[8,32]{1,0:T(8,128)} %len_hbm.1, f32[1,6144]{1,0:T(1,128)} %bitcast.4, f32[16,128]{1,0:T(8,128)} %constant.2.clone.tab_hbm, bf16[256,1536]{1,0:T(8,128)(2,1)} %roll_hbm.1, bf16[6144,256]{1,0:T(8,128)(2,1)} %w_in.1, bf16[64,6144]{1,0:T(8,128)(2,1)} %bitcast.3, ...), custom_call_target="tpu_custom_call" | custom-call | tf_op jit(solution)/shard_map/pallas_call | solution.py:478
  60.1 2.1 %copy.10 = bf16[256,1536]{1,0:T(8,128)(2,1)} copy(bf16[256,1536]{1,0:T(8,128)(2,1)} %shard_map.82) | data formatting | bytes 1572864
where the time goes:
time: 62.3 us; the launch traced here: 62.2 us
  Pallas kernels  60.1 us (96%)
  local copies, waits for them, and re-layouts  2.06 us (3%)
    pallas_call x1, Pallas kernels, fused_body(): pl.pallas_call(functools.partial(fused_kernel, (n_dp, n_t, length, feat,...  60.1 us
    unnamed x1, local copies, waits for them, and re-layouts  2.06 us

commit v1 on v0

--- a/solution.py
+++ b/solution.py
@@ -100,7 +100,7 @@
 
 MESH = pl.DeviceIdType.MESH
 CORES = 2
-HALO = 16
+SIDE = 2
 
 
 def aligned(index, size):
@@ -109,8 +109,9 @@
 
 def fused_kernel(
     cfg, pk_hbm, len_hbm, gain_hbm, tab_hbm, roll_hbm, w_in, k_in, o_in, out,
-    pk_buf, len_buf, gain, tab, wbuf, kbuf, obuf, roll_in, sendb, recvb, packed, scaled, q_part, kv_part, q_recv, kv_recv, ctx,
-    pos_buf, valid_buf, acc, sq_part, sq_recv, send_sems, recv_sems, local_sems,
+    pk_buf, len_buf, gain, tab, wbuf, kbuf, obuf, roll_in, sendb, recvb, packed, scaled, q_rot, kv_part, kv_recv, kv_all, ctx,
+    pos_buf, valid_buf, cos_buf, sin_buf, inv_buf, mask_buf, fold_buf, sq_part, sq_recv, score_part, score_recv,
+    send_sems, recv_sems, local_sems,
 ):
     n_dp, n_t, length, feat, per_source = cfg
     chips = n_dp // CORES
@@ -123,17 +124,29 @@
     most = length // per_source
     rows = length // n_t
     qd = w_in.shape[1]
+    heads = n_t * qd // HD
+    half = length // 2
     me = lax.axis_index("dp")
     t = lax.axis_index("tensor")
     core = lax.rem(me, CORES)
     chip = lax.div(me, CORES)
     partner = chip * CORES + (CORES - 1 - core)
+    near_x = chip + 1 - 2 * lax.rem(chip, SIDE)
+    near_y = chip + SIDE - 2 * SIDE * lax.div(chip, SIDE)
+    first_chip = near_x + core * (near_y - near_x)
+    other_chip = near_y + core * (near_x - near_y)
+    far_chip = chips - 1 - chip
 
     def t_at(k):
         return lax.rem(t + k, n_t)
 
-    def chip_at(k):
-        return lax.rem(chip + k, chips) * CORES + core
+    barrier = pltpu.get_barrier_semaphore()
+    for k in range(1, n_dp):
+        pl.semaphore_signal(
+            barrier, inc=1, device_id=(lax.rem(me + k, n_dp), t), device_id_type=MESH
+        )
+    for k in range(1, n_t):
+        pl.semaphore_signal(barrier, inc=1, device_id=(me, t_at(k)), device_id_type=MESH)
 
     small = [
         pltpu.make_async_copy(source, target, local_sems.at[4 + i])
@@ -147,17 +160,19 @@
         )
     ]
     load = pltpu.make_async_copy(roll_hbm, roll_in, local_sems.at[2])
-    for copy in [*small, load]:
+    own_w = pltpu.make_async_copy(
+        w_in.at[pl.ds(aligned(t, feat), feat)], wbuf.at[t], local_sems.at[0]
+    )
+    own_k = pltpu.make_async_copy(
+        k_in.at[:, pl.ds(aligned(t, feat), feat)],
+        kbuf.at[pl.ds(aligned(t, kd), kd)],
+        local_sems.at[3],
+    )
+    own_o = pltpu.make_async_copy(
+        o_in.at[:, pl.ds(aligned(t, feat), feat)], obuf.at[t], local_sems.at[1]
+    )
+    for copy in [*small, load, own_k, own_w, own_o]:
         copy.start()
-
-    barrier = pltpu.get_barrier_semaphore()
-    for k in range(1, n_dp):
-        pl.semaphore_signal(
-            barrier, inc=1, device_id=(lax.rem(me + k, n_dp), t), device_id_type=MESH
-        )
-    for k in range(1, n_t):
-        pl.semaphore_signal(barrier, inc=1, device_id=(me, t_at(k)), device_id_type=MESH)
-    pl.semaphore_wait(barrier, n_dp + n_t - 2)
 
     started = []
 
@@ -185,44 +200,6 @@
 
     def o_at(u, h, c):
         return obuf.at[u, pl.ds(aligned(h * CORES + c, o_sub), o_sub)]
-
-    w_first, k_first, o_first = {}, {}, {}
-    for k in range(1, n_t):
-        to = t_at(k)
-        k_first[k] = send(
-            k_in.at[
-                pl.ds(aligned(chip, k_rows), k_rows),
-                pl.ds(aligned(to * CORES + core, k_cols), k_cols),
-            ],
-            k_at(t, chip, core),
-            (me, to),
-        )
-    for k in range(1, n_t):
-        to = t_at(k)
-        w_first[k] = send(
-            w_in.at[pl.ds(aligned(to * n_dp + me, w_sub), w_sub)], w_at(t, chip, core), (me, to)
-        )
-    own_w = pltpu.make_async_copy(
-        w_in.at[pl.ds(aligned(t, feat), feat)], wbuf.at[t], local_sems.at[0]
-    )
-    own_w.start()
-    own_k = pltpu.make_async_copy(
-        k_in.at[:, pl.ds(aligned(t, feat), feat)],
-        kbuf.at[pl.ds(aligned(t, kd), kd)],
-        local_sems.at[3],
-    )
-    own_k.start()
-    for k in range(1, n_t):
-        to = t_at(k)
-        o_first[k] = send(
-            o_in.at[pl.ds(aligned(me, o_sub), o_sub), pl.ds(aligned(to, feat), feat)],
-            o_at(t, chip, core),
-            (me, to),
-        )
-    own_o = pltpu.make_async_copy(
-        o_in.at[:, pl.ds(aligned(t, feat), feat)], obuf.at[t], local_sems.at[1]
-    )
-    own_o.start()
 
     down = lax.broadcasted_iota(jnp.int32, (length, length), 0).astype(jnp.float32)
     across = lax.broadcasted_iota(jnp.int32, (length, length), 1).astype(jnp.float32)
@@ -266,16 +243,6 @@
     token = down_1 - group * most
     row_sent = jnp.where(token < pick(match, q_len_r, 1), pick(match, q_start_r, 1) + token, -1.0)
     take_send = (across == row_sent).astype(jnp.float32).astype(jnp.bfloat16)
-    inside = (owner_r == mine) & (doc_start_r <= down) & (down < doc_start_r + q_len_r)
-    is_valid = pick(inside, 1.0, 1)
-    position = (down_1 - pick(inside, doc_start_r, 1)) * is_valid
-    row_got = jnp.where(
-        is_valid > 0.0, pick(inside, q_src_r * block + slot_r * most, 1) + position, -1.0
-    )
-    take_recv = (across == row_got).astype(jnp.float32).astype(jnp.bfloat16)
-    pos_buf[:HALO, :] = jnp.zeros((HALO, HD), jnp.float32)
-    pos_buf[HALO:, :] = jnp.broadcast_to(position, (length, HD))
-    valid_buf[...] = jnp.broadcast_to(is_valid, (length, HD))
 
     tile = 256
     tiles = feat // tile
@@ -290,37 +257,107 @@
     load.wait()
     lax.fori_loop(0, tiles, send_tile, 0)
 
-    rows_of = {}
+    pl.semaphore_wait(barrier, n_dp + n_t - 2)
+
+    others = range(1, n_t)
+    w_first, k_first, o_first = {}, {}, {}
+    for k in others:
+        to = t_at(k)
+        k_first[k] = send(
+            k_in.at[
+                pl.ds(aligned(chip, k_rows), k_rows),
+                pl.ds(aligned(to * CORES + core, k_cols), k_cols),
+            ],
+            k_at(t, chip, core),
+            (me, to),
+        )
+    rows_of = []
     for k in range(1, n_dp):
         to = lax.rem(me + k, n_dp)
-        rows_of[k] = send(
-            sendb.at[pl.ds(aligned(to, block), block)],
-            recvb.at[pl.ds(aligned(me, block), block)],
-            (to, t),
-        )
+        rows_of.append(
+            send(
+                sendb.at[pl.ds(aligned(to, block), block)],
+                recvb.at[pl.ds(aligned(me, block), block)],
+                (to, t),
+            )
+        )
+    for k in others:
+        to = t_at(k)
+        w_first[k] = send(
+            w_in.at[pl.ds(aligned(to * n_dp + me, w_sub), w_sub)], w_at(t, chip, core), (me, to)
+        )
+
+    def send_o(k):
+        to = t_at(k)
+        o_first[k] = send(
+            o_in.at[pl.ds(aligned(me, o_sub), o_sub), pl.ds(aligned(to, feat), feat)],
+            o_at(t, chip, core),
+            (me, to),
+        )
+
+    send_o(1)
+
     keep = pl.ds(aligned(me, block), block)
     recvb[keep, :] = sendb[keep, :]
+    inside = (owner_r == mine) & (doc_start_r <= down) & (down < doc_start_r + q_len_r)
+    is_valid = pick(inside, 1.0, 1)
+    position = (down_1 - pick(inside, doc_start_r, 1)) * is_valid
+    row_got = jnp.where(
+        is_valid > 0.0, pick(inside, q_src_r * block + slot_r * most, 1) + position, -1.0
+    )
+    take_recv = (across == row_got).astype(jnp.float32).astype(jnp.bfloat16)
+    pos = jnp.broadcast_to(position, (length, HD))
+    pos_buf[...] = pos
+    valid_buf[...] = jnp.broadcast_to(is_valid, (length, HD))
+    cosine = jnp.zeros((length, HD), jnp.float32)
+    sine = jnp.zeros((length, HD), jnp.float32)
+    for m in range(most):
+        at_m = pos == float(m)
+        cosine = jnp.where(at_m, tab[m : m + 1, :], cosine)
+        sine = jnp.where(at_m, tab[most + m : most + m + 1, :], sine)
+    cos_buf[...] = cosine
+    sin_buf[...] = sine
+    mask_buf[...] = ((across <= down) & (across >= down - position)).astype(jnp.float32)
+    fold_down = lax.broadcasted_iota(jnp.int32, (length, HD), 0)
+    fold_across = lax.broadcasted_iota(jnp.int32, (length, HD), 1)
+    fold_buf[...] = (
+        (lax.rem(fold_down, most) == lax.rem(fold_across, most))
+        .astype(jnp.float32)
+        .astype(jnp.bfloat16)
+    )
 
     def spread(at, first, j):
         first[j].wait_recv()
         ref = at(t_at(n_t - j), chip, core)
-        return [send(ref, ref, (chip_at(k), t)) for k in range(1, chips)]
-
-    def share(at, hops, j):
-        last = []
-        for k in range(chips):
-            if k:
-                hops[k - 1].wait_recv()
-            ref = at(t_at(n_t - j), lax.rem(chip + chips - k, chips), core)
-            last.append(send(ref, ref, (partner, t)))
-        return last
-
-    others = range(1, n_t)
+        return [
+            send(ref, ref, (first_chip * CORES + core, t)),
+            send(ref, ref, (other_chip * CORES + core, t)),
+            send(ref, ref, (partner, t)),
+        ]
+
+    def relay(at, hops, j):
+        hops[0].wait_recv()
+        ref = at(t_at(n_t - j), first_chip, core)
+        hops.append(send(ref, ref, (other_chip * CORES + core, t)))
+        hops.append(send(ref, ref, (partner, t)))
+
+    def settle(at, hops, j):
+        for near, source in ((1, other_chip), (3, far_chip)):
+            hops[near].wait_recv()
+            ref = at(t_at(n_t - j), source, core)
+            hops.append(send(ref, ref, (partner, t)))
+
+    def finish(hops):
+        for at in (2, 4, 5, 6):
+            hops[at].wait_recv()
+
     k_hops = {j: spread(k_at, k_first, j) for j in others}
+    for j in others:
+        relay(k_at, k_hops[j], j)
     w_hops = {1: spread(w_at, w_first, 1)}
 
-    for k in range(1, n_dp):
-        rows_of[k].wait_recv()
+    for copy in rows_of:
+        copy.wait_recv()
 
     def pack_tile(i, total):
         at = pl.ds(aligned(i, tile), tile)
@@ -331,130 +368,165 @@
         return total + jnp.sum(x * x, axis=1, keepdims=True)
 
     squares = lax.fori_loop(0, tiles, pack_tile, jnp.zeros((length, 1), jnp.float32))
-    kv_part[:HALO, :] = jnp.zeros((HALO, 2 * HD), jnp.bfloat16)
     sq_part[...] = jnp.broadcast_to(pick(diagonal, squares, 0), (8, length))
-    shares = []
-
-    def reduce_rows(part_ref, recv_ref, extra, cols):
+    sq_sent = [send(sq_part, sq_recv.at[k - 1], (me, t_at(k))) for k in others]
+
+    for j in others:
+        settle(k_at, k_hops[j], j)
+    own_k.wait()
+    for j in others:
+        finish(k_hops[j])
+    kv_sent = []
+    for c in range(2):
+        cols = slice(c * HD, (c + 1) * HD)
+        kv_part[:, cols] = lax.dot_general(
+            scaled[...], kbuf[cols, :], (((1,), (1,)), ((), ())),
+            preferred_element_type=jnp.float32,
+        ).astype(jnp.bfloat16)
         for k in others:
             to = t_at(k)
-            shares.append(
+            kv_sent.append(
                 send(
-                    part_ref.at[pl.ds(aligned(to, rows), rows + extra), cols],
-                    recv_ref.at[k - 1, :, cols],
+                    kv_part.at[pl.ds(aligned(to, rows), rows), cols],
+                    kv_recv.at[k - 1, :, cols],
                     (me, to),
                 )
             )
-
-    def project(j):
-        u = t_at(n_t - j)
-        cols = pl.ds(aligned(u, qd), qd)
-        q_part[:, cols] = jnp.dot(
-            scaled[...], wbuf[u], preferred_element_type=jnp.float32
-        ).astype(jnp.bfloat16)
-        reduce_rows(q_part, q_recv, 0, cols)
-
-    own_w.wait()
-    own_k.wait()
-    for k in others:
-        shares.append(send(sq_part, sq_recv.at[k - 1], (me, t_at(k))))
-    project(n_t)
-    for j in others[1:]:
-        w_hops[j] = spread(w_at, w_first, j)
-    k_last = [copy for j in others for copy in share(k_at, k_hops[j], j)]
-    for copy in k_last:
+    send_o(2)
+    relay(w_at, w_hops[1], 1)
+    w_hops[2] = spread(w_at, w_first, 2)
+    relay(w_at, w_hops[2], 2)
+
+    for copy in sq_sent:
         copy.wait_recv()
-    kv_part[HALO:, : 2 * HD] = lax.dot_general(
-        scaled[...], kbuf[...], (((1,), (1,)), ((), ())), preferred_element_type=jnp.float32
-    ).astype(jnp.bfloat16)
-    reduce_rows(kv_part, kv_recv, HALO, pl.ds(0, 2 * HD))
-    w_last = share(w_at, w_hops[1], 1)
-    o_hops = {}
-    for j in others:
-        if j + 1 in w_hops:
-            following = share(w_at, w_hops[j + 1], j + 1)
-        for copy in w_last:
-            copy.wait_recv()
-        w_last = following
-        project(j)
-        o_hops[j] = spread(o_at, o_first, j)
-    for copy in shares:
-        copy.wait_recv()
-
-    keys_at = pl.ds(aligned(t, rows), rows + HALO)
-    queries_at = pl.ds(aligned(t, rows), rows)
-    kv = kv_part[keys_at, :].astype(jnp.float32)
-    for k in range(n_t - 1):
-        kv += kv_recv[k].astype(jnp.float32)
     sq = sq_part[:1, :]
     for k in range(n_t - 1):
         sq += sq_recv[k, :1, :]
-    row_at = lax.broadcasted_iota(jnp.int32, (rows + HALO, length), 0) + (t * rows - HALO)
-    sums = pick(lax.broadcasted_iota(jnp.int32, (rows + HALO, length), 1) == row_at, sq, 1)
-    inverse = lax.rsqrt(sums / (feat * n_t) + epsilon)
-    kv_bf = (kv[:, : 2 * HD] * inverse).astype(jnp.bfloat16)
-    values = kv_bf[:, HD:]
-    pos = pos_buf[keys_at, :]
-    cosine = jnp.zeros((rows + HALO, HD), jnp.float32)
-    sine = jnp.zeros((rows + HALO, HD), jnp.float32)
-    for m in range(most):
-        at_m = pos == float(m)
-        cosine = jnp.where(at_m, tab[m : m + 1, :], cosine)
-        sine = jnp.where(at_m, tab[most + m : most + m + 1, :], sine)
+    inverse = lax.rsqrt(sq / (feat * n_t) + epsilon)
+    inv_buf[...] = jnp.broadcast_to(pick(diagonal, inverse, 1), (length, HD))
 
     def turn(v, c, s):
         return v * c + pltpu.roll(v, HD // 2, 1) * s
 
-    k_rot = turn(kv_bf[:, :HD].astype(jnp.float32), cosine, sine).astype(jnp.bfloat16)
-    q_down = lax.broadcasted_iota(jnp.int32, (rows, rows + HALO), 0).astype(jnp.float32)
-    k_across = lax.broadcasted_iota(jnp.int32, (rows, rows + HALO), 1).astype(jnp.float32) - HALO
-    allowed = (k_across <= q_down) & (k_across >= q_down - pos[HALO:, :1])
+    def project(u):
+        q = jnp.dot(scaled[...], wbuf[u], preferred_element_type=jnp.float32)
+        for h in range(qd // HD):
+            part_q = q[:, h * HD : (h + 1) * HD] * inv_buf[...]
+            q_rot[:, pl.ds(aligned(u * (qd // HD) + h, HD), HD)] = turn(
+                part_q, cos_buf[...], sin_buf[...]
+            ).astype(jnp.bfloat16)
+
+    own_w.wait()
+    project(t)
+
+    mine_rows = pl.ds(aligned(t, rows), rows)
     gathers = []
-    heads = q_part.shape[1] // HD
+    for c in range(2):
+        cols = slice(c * HD, (c + 1) * HD)
+        for copy in kv_sent[c * (n_t - 1) : (c + 1) * (n_t - 1)]:
+            copy.wait_recv()
+        kv = kv_part[mine_rows, cols].astype(jnp.float32)
+        for k in range(n_t - 1):
+            kv += kv_recv[k, :, cols].astype(jnp.float32)
+        kv = (kv * inv_buf[mine_rows, :]).astype(jnp.bfloat16)
+        if c == 0:
+            kv = turn(
+                kv.astype(jnp.float32), cos_buf[mine_rows, :], sin_buf[mine_rows, :]
+            ).astype(jnp.bfloat16)
+        kv_all[mine_rows, cols] = kv
+        at = kv_all.at[mine_rows, cols]
+        gathers.append([send(at, at, (me, t_at(k))) for k in others])
+    send_o(3)
+
+    w_hops[3] = spread(w_at, w_first, 3)
+    relay(w_at, w_hops[3], 3)
+    o_hops = {1: spread(o_at, o_first, 1)}
+    for j in others:
+        settle(w_at, w_hops[j], j)
+        finish(w_hops[j])
+        project(t_at(n_t - j))
+        if j == 1:
+            o_hops[2] = spread(o_at, o_first, 2)
+        if j == 2:
+            relay(o_at, o_hops[1], 1)
+
+    for copy in gathers[0]:
+        copy.wait_recv()
+    lane = lax.broadcasted_iota(jnp.int32, (half, HD), 1)
+    line = lax.broadcasted_iota(jnp.int32, (half, HD), 0)
+    cell = lax.div(lane, most)
+    compact = jnp.zeros((half, HD), jnp.float32)
     for h in range(heads):
-        cols = slice(h * HD, (h + 1) * HD)
-        q = q_part[queries_at, cols].astype(jnp.float32)
-        for k in range(n_t - 1):
-            q += q_recv[k, :, cols].astype(jnp.float32)
-        q_rot = turn(q * inverse[HALO:], cosine[HALO:], sine[HALO:]).astype(jnp.bfloat16)
         scores = lax.dot_general(
-            q_rot, k_rot, (((1,), (1,)), ((), ())), preferred_element_type=jnp.float32
-        ) * (1.0 / math.sqrt(HD))
-        scores = jnp.where(allowed, scores, -jnp.inf)
-        exponent = jnp.exp(scores - jnp.max(scores, axis=1, keepdims=True))
-        weights = (exponent / jnp.sum(exponent, axis=1, keepdims=True)).astype(jnp.bfloat16)
-        ctx[queries_at, cols] = jnp.dot(
-            weights, values, preferred_element_type=jnp.float32
+            q_rot[:, h * HD : (h + 1) * HD], kv_all[:, :HD], (((1,), (1,)), ((), ())),
+            preferred_element_type=jnp.float32,
+        )
+        scores = (scores * mask_buf[...]).astype(jnp.bfloat16)
+        folded = jnp.dot(scores, fold_buf[...], preferred_element_type=jnp.float32)
+        compact = jnp.where(cell == h, folded[:half], compact)
+        compact = jnp.where(cell == heads + h, folded[half:], compact)
+    score_part[...] = compact.astype(jnp.bfloat16)
+    score_sent = [send(score_part, score_recv.at[k - 1], (me, t_at(k))) for k in others]
+
+    o_hops[3] = spread(o_at, o_first, 3)
+    relay(o_at, o_hops[2], 2)
+    relay(o_at, o_hops[3], 3)
+    for j in others:
+        settle(o_at, o_hops[j], j)
+
+    for copy in score_sent:
+        copy.wait_recv()
+    total = score_part[...].astype(jnp.float32)
+    for k in range(n_t - 1):
+        total += score_recv[k].astype(jnp.float32)
+    place = jnp.where(cell < heads, pos_buf[:half, :], pos_buf[half:, :])
+    back = lax.rem(line - lane + HD, most).astype(jnp.float32)
+    total = jnp.where(back <= place, total * (1.0 / math.sqrt(HD)), -jnp.inf)
+
+    def around(value, combine):
+        step = 1
+        while step < most:
+            low = lax.rem(lax.div(lane, step), 2) == 0
+            value = combine(
+                value,
+                jnp.where(low, pltpu.roll(value, HD - step, 1), pltpu.roll(value, step, 1)),
+            )
+            step *= 2
+        return value
+
+    exponent = jnp.exp(total - around(total, jnp.maximum))
+    weights = exponent / around(exponent, jnp.add)
+    for copy in gathers[1]:
+        copy.wait_recv()
+    for h in range(heads):
+        chosen_w = jnp.concatenate(
+            [jnp.where(cell == h, weights, 0.0), jnp.where(cell == heads + h, weights, 0.0)], axis=0
         ).astype(jnp.bfloat16)
-        if (h + 1) % (heads // n_t) == 0:
-            at = ctx.at[queries_at, pl.ds((h + 1 - heads // n_t) * HD, heads // n_t * HD)]
-            for k in others:
-                gathers.append(send(at, at, (me, t_at(k))))
-
-    o_last = [copy for j in others for copy in share(o_at, o_hops[j], j)]
+        dense = lax.dot_general(
+            chosen_w, fold_buf[...], (((1,), (1,)), ((), ())), preferred_element_type=jnp.float32
+        )
+        dense = (dense * mask_buf[...]).astype(jnp.bfloat16)
+        ctx[:, h * HD : (h + 1) * HD] = jnp.dot(
+            dense, kv_all[:, HD:], preferred_element_type=jnp.float32
+        ).astype(jnp.bfloat16)
+
     own_o.wait()
-    for copy in o_last:
-        copy.wait_recv()
-
-    for u in range(n_t):
-        for copy in gathers[u * (n_t - 1) : (u + 1) * (n_t - 1)]:
-            copy.wait_recv()
-
-        def out_tile(i, carry, u=u):
-            at = pl.ds(aligned(i, tile), tile)
-            total = packed[:, at].astype(jnp.float32) if u == 0 else acc[:, at]
-            total += jnp.dot(
+    for j in others:
+        finish(o_hops[j])
+
+    def out_tile(i, carry):
+        at = pl.ds(aligned(i, tile), tile)
+        result = packed[:, at].astype(jnp.float32)
+        for u in range(n_t):
+            result += jnp.dot(
                 ctx[:, u * o_rows : (u + 1) * o_rows],
                 obuf[u, :, at],
                 preferred_element_type=jnp.float32,
             )
-            if u < n_t - 1:
-                acc[:, at] = total
-            else:
-                out[:, at] = jnp.where(valid_buf[:, :1] > 0.0, total, 0.0).astype(jnp.bfloat16)
-            return carry
-
-        lax.fori_loop(0, tiles, out_tile, 0)
+        out[:, at] = jnp.where(valid_buf[:, :1] > 0.0, result, 0.0).astype(jnp.bfloat16)
+        return carry
+
+    lax.fori_loop(0, tiles, out_tile, 0)
     for copy in started:
         copy.wait_send()
 
@@ -471,7 +543,7 @@
     sin_tab = np.concatenate([-np.sin(angles), np.sin(angles)], axis=1).astype(np.float32)
     rows = length // n_t
     chips = n_dp // CORES
-    copies = 3 * (n_t - 1) * (1 + chips - 1 + chips) + (n_dp - 1) + (2 + 2 * n_t) * (n_t - 1)
+    copies = 3 * (n_t - 1) * (1 + chips - 1 + chips) + (n_dp - 1) + 6 * (n_t - 1)
     vmem = pl.BlockSpec(memory_space=pltpu.VMEM)
     hbm = pl.BlockSpec(memory_space=pl.ANY)
     bf, f32 = jnp.bfloat16, jnp.float32
@@ -494,15 +566,21 @@
             pltpu.VMEM((length, feat), bf),
             pltpu.VMEM((length, feat), bf),
             pltpu.VMEM((length, n_t * qd), bf),
-            pltpu.VMEM((length + HALO, 2 * HD), bf),
-            pltpu.VMEM((n_t - 1, rows, n_t * qd), bf),
-            pltpu.VMEM((n_t - 1, rows + HALO, 2 * HD), bf),
+            pltpu.VMEM((length, 2 * HD), bf),
+            pltpu.VMEM((n_t - 1, rows, 2 * HD), bf),
+            pltpu.VMEM((length, 2 * HD), bf),
             pltpu.VMEM((length, n_t * qd), bf),
-            pltpu.VMEM((length + HALO, HD), f32),
             pltpu.VMEM((length, HD), f32),
-            pltpu.VMEM((length, feat), f32),
+            pltpu.VMEM((length, HD), f32),
+            pltpu.VMEM((length, HD), f32),
+            pltpu.VMEM((length, HD), f32),
+            pltpu.VMEM((length, HD), f32),
+            pltpu.VMEM((length, length), f32),
+            pltpu.VMEM((length, HD), bf),
             pltpu.VMEM((8, length), f32),
             pltpu.VMEM((n_t - 1, 8, length), f32),
+            pltpu.VMEM((length // 2, HD), bf),
+            pltpu.VMEM((n_t - 1, length // 2, HD), bf),
             pltpu.SemaphoreType.DMA((copies,)),
             pltpu.SemaphoreType.DMA((copies,)),
             pltpu.SemaphoreType.DMA((8,)),
@@ -520,18 +598,24 @@
 def body(rollout, lengths, packing, norm_gain, query_weight, keyval_weight, out_weight):
     n_dp, n_t = lax.axis_size("dp"), lax.axis_size("tensor")
     length, feat = rollout.shape
+    per_source = lengths.shape[1]
     qd, kd = query_weight.shape[1], keyval_weight.shape[1]
     fits = (
         kd * n_t == 2 * HD
         and n_t == 4
-        and kd % (HALO * n_dp // CORES) == 0
+        and n_dp == SIDE * SIDE * CORES
+        and qd % HD == 0
+        and n_t * qd // HD <= GROUP
+        and per_source * 8 == length
+        and n_t * qd // HD * 8 * 2 == HD
+        and kd % (16 * n_dp // CORES) == 0
         and feat % (128 * CORES) == 0
-        and n_dp % CORES == 0
-        and length % (n_t * HALO) == 0
+        and length % (n_t * 16) == 0
+        and length == 2 * HD
         and packing.shape[0] == length
-        and (length // n_dp) % HALO == 0
+        and (length // n_dp) % 16 == 0
         and feat % 512 == 0
-        and lengths.shape[1] % n_dp == 0
+        and per_source % n_dp == 0
     )
     chosen = fused_body if fits else plain_body
     return chosen(rollout, lengths, packing, norm_gain, query_weight, keyval_weight, out_weight)

time: 62.3 us -> 54.3 us (0.87)
  Pallas kernels: 60.1 us -> 52.1 us
    pallas_call x1, Pallas kernels: 60.1 us -> 52.1 us  [fused_body(): pl.pallas_call(functools.partial(fused_kernel, (n_dp, n_t, length, feat,...]
where the time goes in v1:
time: 54.3 us; the launch traced here: 54.1 us
  Pallas kernels  52.1 us (96%)
  local copies, waits for them, and re-layouts  2.06 us (4%)
    pallas_call x1, Pallas kernels, fused_body(): pl.pallas_call(functools.partial(fused_kernel, (n_dp, n_t, length, feat,...  52.1 us
    unnamed x1, local copies, waits for them, and re-layouts  2.06 us

profile of v1, /device:TPU:0, one launch (start us, length us, event | category | flops | bytes accessed | tf_op | source)
XLA Modules:
  0.0 54.1 jit_solution(3432707690193901992)
XLA Ops:
  0.0 52.1 %shard_map.82 = bf16[256,1536]{1,0:T(8,128)(2,1)} custom-call(s32[1,256]{1,0:T(1,128)} %bitcast.5, s32[8,32]{1,0:T(8,128)} %len_hbm.1, f32[1,6144]{1,0:T(1,128)} %bitcast.4, f32[16,128]{1,0:T(8,128)} %constant.2.clone.tab_hbm, bf16[256,1536]{1,0:T(8,128)(2,1)} %roll_hbm.1, bf16[6144,256]{1,0:T(8,128)(2,1)} %w_in.1, bf16[64,6144]{1,0:T(8,128)(2,1)} %bitcast.3, ...), custom_call_target="tpu_custom_call" | custom-call | tf_op jit(solution)/shard_map/pallas_call | solution.py:550
  52.1 2.1 %copy.10 = bf16[256,1536]{1,0:T(8,128)(2,1)} copy(bf16[256,1536]{1,0:T(8,128)(2,1)} %shard_map.82) | data formatting | bytes 1572864

commit v2 on v1

--- a/solution.py
+++ b/solution.py
@@ -111,7 +111,7 @@
     cfg, pk_hbm, len_hbm, gain_hbm, tab_hbm, roll_hbm, w_in, k_in, o_in, out,
     pk_buf, len_buf, gain, tab, wbuf, kbuf, obuf, roll_in, sendb, recvb, packed, scaled, q_rot, kv_part, kv_recv, kv_all, ctx,
     pos_buf, valid_buf, cos_buf, sin_buf, inv_buf, mask_buf, fold_buf, sq_part, sq_recv, score_part, score_recv,
-    send_sems, recv_sems, local_sems,
+    send_sem, recv_sems, local_sems,
 ):
     n_dp, n_t, length, feat, per_source = cfg
     chips = n_dp // CORES
@@ -174,21 +174,26 @@
     for copy in [*small, load, own_k, own_w, own_o]:
         copy.start()
 
-    started = []
-
-    def send(source, target, device):
-        at = len(started)
+    started, named = [], []
+
+    def slot():
+        named.append(recv_sems.at[len(named)])
+        return named[-1]
+
+    def send(source, target, device, arrival):
         copy = pltpu.make_async_remote_copy(
             src_ref=source,
             dst_ref=target,
-            send_sem=send_sems.at[at],
-            recv_sem=recv_sems.at[at],
+            send_sem=send_sem,
+            recv_sem=arrival,
             device_id=device,
             device_id_type=MESH,
         )
         copy.start()
         started.append(copy)
-        return copy
+
+    def arrived(ref, arrival):
+        pltpu.make_async_copy(ref, ref, arrival).wait()
 
     def w_at(u, h, c):
         return wbuf.at[u, pl.ds(aligned(h * CORES + c, w_sub), w_sub)]
@@ -246,56 +251,57 @@
 
     tile = 256
     tiles = feat // tile
-
-    def send_tile(i, carry):
-        at = pl.ds(aligned(i, tile), tile)
+    load.wait()
+    for i in range(tiles):
+        at = slice(i * tile, (i + 1) * tile)
         sendb[:, at] = jnp.dot(
             take_send, roll_in[:, at], preferred_element_type=jnp.float32
         ).astype(jnp.bfloat16)
-        return carry
-
-    load.wait()
-    lax.fori_loop(0, tiles, send_tile, 0)
 
     pl.semaphore_wait(barrier, n_dp + n_t - 2)
 
-    others = range(1, n_t)
-    w_first, k_first, o_first = {}, {}, {}
+    others = (1, 3, 2) if n_t == 4 else tuple(range(1, n_t))
+    k_first = slot()
     for k in others:
         to = t_at(k)
-        k_first[k] = send(
+        send(
             k_in.at[
                 pl.ds(aligned(chip, k_rows), k_rows),
                 pl.ds(aligned(to * CORES + core, k_cols), k_cols),
             ],
             k_at(t, chip, core),
             (me, to),
-        )
-    rows_of = []
-    for k in range(1, n_dp):
-        to = lax.rem(me + k, n_dp)
-        rows_of.append(
-            send(
-                sendb.at[pl.ds(aligned(to, block), block)],
-                recvb.at[pl.ds(aligned(me, block), block)],
-                (to, t),
-            )
-        )
+            k_first,
+        )
+    row_group = slot()
+
+    def send_rows(to):
+        send(
+            sendb.at[pl.ds(aligned(to, block), block)],
+            recvb.at[pl.ds(aligned(me, block), block)],
+            (to, t),
+            row_group,
+        )
+
+    for c in range(CORES):
+        send_rows(far_chip * CORES + lax.rem(core + c, CORES))
+    send_rows(partner)
+    w_first = {k: slot() for k in others}
+    o_first = {k: slot() for k in others}
     for k in others:
         to = t_at(k)
-        w_first[k] = send(
-            w_in.at[pl.ds(aligned(to * n_dp + me, w_sub), w_sub)], w_at(t, chip, core), (me, to)
-        )
-
-    def send_o(k):
+        send(
+            w_in.at[pl.ds(aligned(to * n_dp + me, w_sub), w_sub)], w_at(t, chip, core), (me, to),
+            w_first[k],
+        )
+    for k in others:
         to = t_at(k)
-        o_first[k] = send(
+        send(
             o_in.at[pl.ds(aligned(me, o_sub), o_sub), pl.ds(aligned(to, feat), feat)],
             o_at(t, chip, core),
             (me, to),
-        )
-
-    send_o(1)
+            o_first[k],
+        )
 
     keep = pl.ds(aligned(me, block), block)
     recvb[keep, :] = sendb[keep, :]
@@ -326,57 +332,96 @@
         .astype(jnp.bfloat16)
     )
 
-    def spread(at, first, j):
-        first[j].wait_recv()
+    first_dev = first_chip * CORES + core
+    other_dev = other_chip * CORES + core
+
+    def spread(at, j, hops):
         ref = at(t_at(n_t - j), chip, core)
-        return [
-            send(ref, ref, (first_chip * CORES + core, t)),
-            send(ref, ref, (other_chip * CORES + core, t)),
-            send(ref, ref, (partner, t)),
-        ]
-
-    def relay(at, hops, j):
-        hops[0].wait_recv()
+        send(ref, ref, (first_dev, t), hops[0])
+        send(ref, ref, (other_dev, t), hops[1])
+        send(ref, ref, (partner, t), hops[2])
+
+    def relay(at, j, hops):
         ref = at(t_at(n_t - j), first_chip, core)
-        hops.append(send(ref, ref, (other_chip * CORES + core, t)))
-        hops.append(send(ref, ref, (partner, t)))
-
-    def settle(at, hops, j):
-        for near, source in ((1, other_chip), (3, far_chip)):
-            hops[near].wait_recv()
+        send(ref, ref, (other_dev, t), hops[1])
+        send(ref, ref, (partner, t), hops[2])
+
+    def settle(at, j, hops):
+        for source in (other_chip, far_chip):
             ref = at(t_at(n_t - j), source, core)
-            hops.append(send(ref, ref, (partner, t)))
-
-    def finish(hops):
-        for at in (2, 4, 5, 6):
-            hops[at].wait_recv()
-
-    k_hops = {j: spread(k_at, k_first, j) for j in others}
+            send(ref, ref, (partner, t), hops[2])
+
+    k_hops = [slot() for _ in range(3)]
+    w_hops = {j: [slot() for _ in range(3)] for j in others}
+    o_hops = {j: [slot() for _ in range(3)] for j in others}
+
+    def k_wait(count, arrival):
+        arrived(
+            kbuf.at[pl.ds(0, count * k_rows), pl.ds(0, k_cols)], arrival
+        )
+
+    def w_wait(count, j, arrival):
+        arrived(wbuf.at[t_at(n_t - j), pl.ds(0, count * w_sub)], arrival)
+
+    def o_wait(count, j, arrival):
+        arrived(obuf.at[t_at(n_t - j), pl.ds(0, count * o_sub)], arrival)
+
+    def w_spread(j):
+        w_wait(1, j, w_first[j])
+        spread(w_at, j, w_hops[j])
+
+    def w_relay(j):
+        w_wait(1, j, w_hops[j][0])
+        relay(w_at, j, w_hops[j])
+
+    def w_settle(j):
+        w_wait(2, j, w_hops[j][1])
+        settle(w_at, j, w_hops[j])
+
+    def o_spread(j):
+        o_wait(1, j, o_first[j])
+        spread(o_at, j, o_hops[j])
+
+    def o_relay(j):
+        o_wait(1, j, o_hops[j][0])
+        relay(o_at, j, o_hops[j])
+
+    def o_settle(j):
+        o_wait(2, j, o_hops[j][1])
+        settle(o_at, j, o_hops[j])
+
+    one, three, two = others
+    k_wait(n_t - 1, k_first)
     for j in others:
-        relay(k_at, k_hops[j], j)
-    w_hops = {1: spread(w_at, w_first, 1)}
-
-    for copy in rows_of:
-        copy.wait_recv()
-
-    def pack_tile(i, total):
-        at = pl.ds(aligned(i, tile), tile)
+        spread(k_at, j, k_hops)
+    for near in (first_chip, other_chip):
+        for c in range(CORES):
+            send_rows(near * CORES + lax.rem(core + c, CORES))
+    k_wait(n_t - 1, k_hops[0])
+    for j in others:
+        relay(k_at, j, k_hops)
+    w_spread(one)
+    arrived(recvb.at[pl.ds(0, (n_dp - 1) * block)], row_group)
+    w_spread(three)
+    squares = jnp.zeros((length, 1), jnp.float32)
+    for i in range(tiles):
+        at = slice(i * tile, (i + 1) * tile)
         x = jnp.dot(take_recv, recvb[:, at], preferred_element_type=jnp.float32)
         packed[:, at] = x.astype(jnp.bfloat16)
-        g = gain[:, at]
-        scaled[:, at] = (x * g).astype(jnp.bfloat16)
-        return total + jnp.sum(x * x, axis=1, keepdims=True)
-
-    squares = lax.fori_loop(0, tiles, pack_tile, jnp.zeros((length, 1), jnp.float32))
+        scaled[:, at] = (x * gain[:, at]).astype(jnp.bfloat16)
+        squares += jnp.sum(x * x, axis=1, keepdims=True)
     sq_part[...] = jnp.broadcast_to(pick(diagonal, squares, 0), (8, length))
-    sq_sent = [send(sq_part, sq_recv.at[k - 1], (me, t_at(k))) for k in others]
-
+    sq_group = slot()
+    for k in others:
+        send(sq_part, sq_recv.at[k - 1], (me, t_at(k)), sq_group)
+    w_spread(two)
+    w_relay(one)
+    k_wait(2 * (n_t - 1), k_hops[1])
     for j in others:
-        settle(k_at, k_hops[j], j)
+        settle(k_at, j, k_hops)
     own_k.wait()
-    for j in others:
-        finish(k_hops[j])
-    kv_sent = []
+    k_wait(chips * (n_t - 1), k_hops[2])
+    kv_groups = [slot() for _ in range(2)]
     for c in range(2):
         cols = slice(c * HD, (c + 1) * HD)
         kv_part[:, cols] = lax.dot_general(
@@ -385,20 +430,13 @@
         ).astype(jnp.bfloat16)
         for k in others:
             to = t_at(k)
-            kv_sent.append(
-                send(
-                    kv_part.at[pl.ds(aligned(to, rows), rows), cols],
-                    kv_recv.at[k - 1, :, cols],
-                    (me, to),
-                )
+            send(
+                kv_part.at[pl.ds(aligned(to, rows), rows), cols],
+                kv_recv.at[k - 1, :, cols],
+                (me, to),
+                kv_groups[c],
             )
-    send_o(2)
-    relay(w_at, w_hops[1], 1)
-    w_hops[2] = spread(w_at, w_first, 2)
-    relay(w_at, w_hops[2], 2)
-
-    for copy in sq_sent:
-        copy.wait_recv()
+    arrived(sq_recv, sq_group)
     sq = sq_part[:1, :]
     for k in range(n_t - 1):
         sq += sq_recv[k, :1, :]
@@ -418,13 +456,17 @@
 
     own_w.wait()
     project(t)
+    w_relay(three)
+    w_relay(two)
+    o_spread(one)
+    o_spread(three)
 
     mine_rows = pl.ds(aligned(t, rows), rows)
-    gathers = []
-    for c in range(2):
+    all_groups = [slot() for _ in range(2)]
+
+    def share_kv(c):
         cols = slice(c * HD, (c + 1) * HD)
-        for copy in kv_sent[c * (n_t - 1) : (c + 1) * (n_t - 1)]:
-            copy.wait_recv()
+        arrived(kv_recv.at[:, :, cols], kv_groups[c])
         kv = kv_part[mine_rows, cols].astype(jnp.float32)
         for k in range(n_t - 1):
             kv += kv_recv[k, :, cols].astype(jnp.float32)
@@ -435,23 +477,24 @@
             ).astype(jnp.bfloat16)
         kv_all[mine_rows, cols] = kv
         at = kv_all.at[mine_rows, cols]
-        gathers.append([send(at, at, (me, t_at(k))) for k in others])
-    send_o(3)
-
-    w_hops[3] = spread(w_at, w_first, 3)
-    relay(w_at, w_hops[3], 3)
-    o_hops = {1: spread(o_at, o_first, 1)}
-    for j in others:
-        settle(w_at, w_hops[j], j)
-        finish(w_hops[j])
-        project(t_at(n_t - j))
-        if j == 1:
-            o_hops[2] = spread(o_at, o_first, 2)
-        if j == 2:
-            relay(o_at, o_hops[1], 1)
-
-    for copy in gathers[0]:
-        copy.wait_recv()
+        for k in others:
+            send(at, at, (me, t_at(k)), all_groups[c])
+
+    share_kv(0)
+    w_settle(one)
+    w_wait(chips, one, w_hops[one][2])
+    project(t_at(n_t - one))
+    o_relay(one)
+    share_kv(1)
+    w_settle(three)
+    w_wait(chips, three, w_hops[three][2])
+    project(t_at(n_t - three))
+    o_spread(two)
+    w_settle(two)
+    w_wait(chips, two, w_hops[two][2])
+    project(t_at(n_t - two))
+    o_relay(three)
+    arrived(kv_all.at[pl.ds(0, (n_t - 1) * rows), pl.ds(0, HD)], all_groups[0])
     lane = lax.broadcasted_iota(jnp.int32, (half, HD), 1)
     line = lax.broadcasted_iota(jnp.int32, (half, HD), 0)
     cell = lax.div(lane, most)
@@ -466,16 +509,15 @@
         compact = jnp.where(cell == h, folded[:half], compact)
         compact = jnp.where(cell == heads + h, folded[half:], compact)
     score_part[...] = compact.astype(jnp.bfloat16)
-    score_sent = [send(score_part, score_recv.at[k - 1], (me, t_at(k))) for k in others]
-
-    o_hops[3] = spread(o_at, o_first, 3)
-    relay(o_at, o_hops[2], 2)
-    relay(o_at, o_hops[3], 3)
+    score_group = slot()
+    for k in others:
+        send(score_part, score_recv.at[k - 1], (me, t_at(k)), score_group)
+
+    o_relay(two)
     for j in others:
-        settle(o_at, o_hops[j], j)
-
-    for copy in score_sent:
-        copy.wait_recv()
+        o_settle(j)
+
+    arrived(score_recv, score_group)
     total = score_part[...].astype(jnp.float32)
     for k in range(n_t - 1):
         total += score_recv[k].astype(jnp.float32)
@@ -496,8 +538,7 @@
 
     exponent = jnp.exp(total - around(total, jnp.maximum))
     weights = exponent / around(exponent, jnp.add)
-    for copy in gathers[1]:
-        copy.wait_recv()
+    arrived(kv_all.at[pl.ds(0, (n_t - 1) * rows), pl.ds(HD, HD)], all_groups[1])
     for h in range(heads):
         chosen_w = jnp.concatenate(
             [jnp.where(cell == h, weights, 0.0), jnp.where(cell == heads + h, weights, 0.0)], axis=0
@@ -512,10 +553,10 @@
 
     own_o.wait()
     for j in others:
-        finish(o_hops[j])
-
-    def out_tile(i, carry):
-        at = pl.ds(aligned(i, tile), tile)
+        o_wait(chips, j, o_hops[j][2])
+
+    for i in range(tiles):
+        at = slice(i * tile, (i + 1) * tile)
         result = packed[:, at].astype(jnp.float32)
         for u in range(n_t):
             result += jnp.dot(
@@ -524,9 +565,6 @@
                 preferred_element_type=jnp.float32,
             )
         out[:, at] = jnp.where(valid_buf[:, :1] > 0.0, result, 0.0).astype(jnp.bfloat16)
-        return carry
-
-    lax.fori_loop(0, tiles, out_tile, 0)
     for copy in started:
         copy.wait_send()
 
@@ -542,10 +580,9 @@
     cos_tab = np.concatenate([np.cos(angles)] * 2, axis=1).astype(np.float32)
     sin_tab = np.concatenate([-np.sin(angles), np.sin(angles)], axis=1).astype(np.float32)
     rows = length // n_t
-    chips = n_dp // CORES
-    copies = 3 * (n_t - 1) * (1 + chips - 1 + chips) + (n_dp - 1) + 6 * (n_t - 1)
+    groups = 4 + 8 * (n_t - 1) + 7
     vmem = pl.BlockSpec(memory_space=pltpu.VMEM)
-    hbm = pl.BlockSpec(memory_space=pl.ANY)
+    hbm = pl.BlockSpec(memory_space=pltpu.HBM)
     bf, f32 = jnp.bfloat16, jnp.float32
     return pl.pallas_call(
         functools.partial(fused_kernel, (n_dp, n_t, length, feat, per_source)),
@@ -581,17 +618,22 @@
             pltpu.VMEM((n_t - 1, 8, length), f32),
             pltpu.VMEM((length // 2, HD), bf),
             pltpu.VMEM((n_t - 1, length // 2, HD), bf),
-            pltpu.SemaphoreType.DMA((copies,)),
-            pltpu.SemaphoreType.DMA((copies,)),
+            pltpu.SemaphoreType.DMA,
+            pltpu.SemaphoreType.DMA((groups,)),
             pltpu.SemaphoreType.DMA((8,)),
         ],
         compiler_params=pltpu.CompilerParams(
-            collective_id=0, has_side_effects=True, vmem_limit_bytes=60 * 1024 * 1024
+            collective_id=0, has_side_effects=True, vmem_limit_bytes=32 * 1024 * 1024
         ),
     )(
-        packing[None, :], lengths, norm_gain[None, :],
-        jnp.asarray(np.concatenate([cos_tab, sin_tab])), rollout, query_weight,
-        keyval_weight.T, out_weight,
+        *(
+            pltpu.with_memory_space_constraint(operand, pltpu.HBM)
+            for operand in (
+                packing[None, :], lengths, norm_gain[None, :],
+                jnp.asarray(np.concatenate([cos_tab, sin_tab])), rollout, query_weight,
+                keyval_weight.T, out_weight,
+            )
+        )
     )
 
 

time: 54.3 us -> 46.4 us (0.85)
  Pallas kernels: 52.1 us -> 45.4 us
  local copies, waits for them, and re-layouts: 2.06 us -> 0.88 us
    pallas_call x1, Pallas kernels: 52.1 us -> 45.4 us  [fused_body(): pl.pallas_call(functools.partial(fused_kernel, (n_dp, n_t, length, feat,...]
    unnamed x1, local copies, waits for them, and re-layouts: 2.06 us -> 0.88 us
where the time goes in v2:
time: 46.4 us; the launch traced here: 46.3 us
  Pallas kernels  45.4 us (98%)
  local copies, waits for them, and re-layouts  0.88 us (2%)
    pallas_call x1, Pallas kernels, fused_body(): pl.pallas_call(functools.partial(fused_kernel, (n_dp, n_t, length, feat,...  45.4 us

profile of v2, /device:TPU:0, one launch (start us, length us, event | category | flops | bytes accessed | tf_op | source)
XLA Modules:
  0.0 46.3 jit_solution(10893024353047103378)
XLA Ops:
  0.0 45.4 %shard_map.82 = bf16[256,1536]{1,0:T(8,128)(2,1)S(1)} custom-call(s32[1,256]{1,0:T(1,128)} %bitcast.5, s32[8,32]{1,0:T(8,128)} %len_hbm.1, f32[1,6144]{1,0:T(1,128)} %bitcast.4, f32[16,128]{1,0:T(8,128)} %constant.2.clone.tab_hbm, bf16[256,1536]{1,0:T(8,128)(2,1)} %roll_hbm.1, bf16[6144,256]{1,0:T(8,128)(2,1)} %w_in.1, bf16[64,6144]{1,0:T(8,128)(2,1)} %bitcast.3, ...), custom_call_target="tpu_custom_call" | custom-call | tf_op jit(solution)/shard_map/pallas_call | solution.py:587
  45.4 0.9 %copy.10 = bf16[256,1536]{1,0:T(8,128)(2,1)} copy(bf16[256,1536]{1,0:T(8,128)(2,1)S(1)} %shard_map.82) | data formatting | bytes 1572864

commit v3 on v2

--- a/solution.py
+++ b/solution.py
@@ -285,16 +285,22 @@
 
     for c in range(CORES):
         send_rows(far_chip * CORES + lax.rem(core + c, CORES))
+    for c in range(CORES):
+        send_rows(first_chip * CORES + lax.rem(core + c, CORES))
     send_rows(partner)
     w_first = {k: slot() for k in others}
     o_first = {k: slot() for k in others}
-    for k in others:
+
+    def send_w(k):
         to = t_at(k)
         send(
             w_in.at[pl.ds(aligned(to * n_dp + me, w_sub), w_sub)], w_at(t, chip, core), (me, to),
             w_first[k],
         )
-    for k in others:
+
+    send_w(1)
+
+    def send_o(k):
         to = t_at(k)
         send(
             o_in.at[pl.ds(aligned(me, o_sub), o_sub), pl.ds(aligned(to, feat), feat)],
@@ -391,16 +397,20 @@
         settle(o_at, j, o_hops[j])
 
     one, three, two = others
+    o_early, o_late = (one, three), (two,)
+    o_a, o_b, o_c = o_early + o_late
     k_wait(n_t - 1, k_first)
     for j in others:
         spread(k_at, j, k_hops)
-    for near in (first_chip, other_chip):
-        for c in range(CORES):
-            send_rows(near * CORES + lax.rem(core + c, CORES))
+    for c in range(CORES):
+        send_rows(other_chip * CORES + lax.rem(core + c, CORES))
+    send_w(three)
+    send_w(two)
+    w_spread(one)
+    send_o(one)
     k_wait(n_t - 1, k_hops[0])
     for j in others:
         relay(k_at, j, k_hops)
-    w_spread(one)
     arrived(recvb.at[pl.ds(0, (n_dp - 1) * block)], row_group)
     w_spread(three)
     squares = jnp.zeros((length, 1), jnp.float32)
@@ -414,6 +424,7 @@
     sq_group = slot()
     for k in others:
         send(sq_part, sq_recv.at[k - 1], (me, t_at(k)), sq_group)
+    send_o(three)
     w_spread(two)
     w_relay(one)
     k_wait(2 * (n_t - 1), k_hops[1])
@@ -436,6 +447,9 @@
                 (me, to),
                 kv_groups[c],
             )
+        if c == 0:
+            send_o(two)
+    w_relay(three)
     arrived(sq_recv, sq_group)
     sq = sq_part[:1, :]
     for k in range(n_t - 1):
@@ -456,11 +470,6 @@
 
     own_w.wait()
     project(t)
-    w_relay(three)
-    w_relay(two)
-    o_spread(one)
-    o_spread(three)
-
     mine_rows = pl.ds(aligned(t, rows), rows)
     all_groups = [slot() for _ in range(2)]
 
@@ -480,20 +489,22 @@
         for k in others:
             send(at, at, (me, t_at(k)), all_groups[c])
 
+    w_relay(two)
+    w_settle(one)
     share_kv(0)
-    w_settle(one)
+    w_settle(three)
+    o_spread(o_a)
     w_wait(chips, one, w_hops[one][2])
     project(t_at(n_t - one))
-    o_relay(one)
-    share_kv(1)
-    w_settle(three)
+    w_settle(two)
+    o_spread(o_b)
     w_wait(chips, three, w_hops[three][2])
     project(t_at(n_t - three))
-    o_spread(two)
-    w_settle(two)
     w_wait(chips, two, w_hops[two][2])
     project(t_at(n_t - two))
-    o_relay(three)
+    share_kv(1)
+    o_relay(o_a)
+    o_spread(o_c)
     arrived(kv_all.at[pl.ds(0, (n_t - 1) * rows), pl.ds(0, HD)], all_groups[0])
     lane = lax.broadcasted_iota(jnp.int32, (half, HD), 1)
     line = lax.broadcasted_iota(jnp.int32, (half, HD), 0)
@@ -513,10 +524,11 @@
     for k in others:
         send(score_part, score_recv.at[k - 1], (me, t_at(k)), score_group)
 
-    o_relay(two)
-    for j in others:
-        o_settle(j)
-
+    o_relay(o_b)
+    o_settle(o_a)
+    o_relay(o_c)
+    o_settle(o_b)
+    o_settle(o_c)
     arrived(score_recv, score_group)
     total = score_part[...].astype(jnp.float32)
     for k in range(n_t - 1):

time: 46.4 us -> 44.1 us (0.950)
  Pallas kernels: 45.4 us -> 43.1 us
    pallas_call x1, Pallas kernels: 45.4 us -> 43.1 us  [fused_body(): pl.pallas_call(functools.partial(fused_kernel, (n_dp, n_t, length, feat,...]
where the time goes in v3:
time: 44.1 us; the launch traced here: 44 us
  Pallas kernels  43.1 us (98%)
  local copies, waits for them, and re-layouts  0.88 us (2%)
    pallas_call x1, Pallas kernels, fused_body(): pl.pallas_call(functools.partial(fused_kernel, (n_dp, n_t, length, feat,...  43.1 us
    unnamed x1, local copies, waits for them, and re-layouts  0.88 us

profile of v3, /device:TPU:0, one launch (start us, length us, event | category | flops | bytes accessed | tf_op | source)
XLA Modules:
  0.0 44.0 jit_solution(15940851413008542984)
XLA Ops:
  0.0 43.1 %shard_map.82 = bf16[256,1536]{1,0:T(8,128)(2,1)S(1)} custom-call(s32[1,256]{1,0:T(1,128)} %bitcast.5, s32[8,32]{1,0:T(8,128)} %len_hbm.1, f32[1,6144]{1,0:T(1,128)} %bitcast.4, f32[16,128]{1,0:T(8,128)} %constant.2.clone.tab_hbm, bf16[256,1536]{1,0:T(8,128)(2,1)} %roll_hbm.1, bf16[6144,256]{1,0:T(8,128)(2,1)} %w_in.1, bf16[64,6144]{1,0:T(8,128)(2,1)} %bitcast.3, ...), custom_call_target="tpu_custom_call" | custom-call | tf_op jit(solution)/shard_map/pallas_call | solution.py:599
  43.1 0.9 %copy.10 = bf16[256,1536]{1,0:T(8,128)(2,1)} copy(bf16[256,1536]{1,0:T(8,128)(2,1)S(1)} %shard_map.82) | data formatting | bytes 1572864

commit v4 on v3

--- a/solution.py
+++ b/solution.py
@@ -110,7 +110,7 @@
 def fused_kernel(
     cfg, pk_hbm, len_hbm, gain_hbm, tab_hbm, roll_hbm, w_in, k_in, o_in, out,
     pk_buf, len_buf, gain, tab, wbuf, kbuf, obuf, roll_in, sendb, recvb, packed, scaled, q_rot, kv_part, kv_recv, kv_all, ctx,
-    pos_buf, valid_buf, cos_buf, sin_buf, inv_buf, mask_buf, fold_buf, sq_part, sq_recv, score_part, score_recv,
+    pos_buf, valid_buf, cos_buf, sin_buf, inv_buf, mask_buf, fold_buf, sq_part, sq_recv, score_part, score_recv, acc,
     send_sem, recv_sems, local_sems,
 ):
     n_dp, n_t, length, feat, per_source = cfg
@@ -202,9 +202,6 @@
         return kbuf.at[
             pl.ds(aligned(u * chips + h, k_rows), k_rows), pl.ds(aligned(c, k_cols), k_cols)
         ]
-
-    def o_at(u, h, c):
-        return obuf.at[u, pl.ds(aligned(h * CORES + c, o_sub), o_sub)]
 
     down = lax.broadcasted_iota(jnp.int32, (length, length), 0).astype(jnp.float32)
     across = lax.broadcasted_iota(jnp.int32, (length, length), 1).astype(jnp.float32)
@@ -289,7 +286,7 @@
         send_rows(first_chip * CORES + lax.rem(core + c, CORES))
     send_rows(partner)
     w_first = {k: slot() for k in others}
-    o_first = {k: slot() for k in others}
+    o_first = [slot() for _ in range(n_t)]
 
     def send_w(k):
         to = t_at(k)
@@ -300,13 +297,25 @@
 
     send_w(1)
 
-    def send_o(k):
-        to = t_at(k)
+    o_parts = ((others[0], 0, 1), (others[1], 0, 1), (others[2], 0, 2), (others[2], 1, 2))
+
+    def o_piece(p):
+        _, index, split = o_parts[p]
+
+        def at(u, h, c):
+            size = o_sub // split
+            return obuf.at[u, pl.ds(aligned((h * CORES + c) * split + index, size), size)]
+
+        return at
+
+    def send_o(p):
+        j, index, split = o_parts[p]
+        to, size = t_at(j), o_sub // split
         send(
-            o_in.at[pl.ds(aligned(me, o_sub), o_sub), pl.ds(aligned(to, feat), feat)],
-            o_at(t, chip, core),
+            o_in.at[pl.ds(aligned(me * split + index, size), size), pl.ds(aligned(to, feat), feat)],
+            o_piece(p)(t, chip, core),
             (me, to),
-            o_first[k],
+            o_first[p],
         )
 
     keep = pl.ds(aligned(me, block), block)
@@ -359,7 +368,7 @@
 
     k_hops = [slot() for _ in range(3)]
     w_hops = {j: [slot() for _ in range(3)] for j in others}
-    o_hops = {j: [slot() for _ in range(3)] for j in others}
+    o_hops = [[slot() for _ in range(3)] for _ in range(n_t)]
 
     def k_wait(count, arrival):
         arrived(
@@ -369,8 +378,9 @@
     def w_wait(count, j, arrival):
         arrived(wbuf.at[t_at(n_t - j), pl.ds(0, count * w_sub)], arrival)
 
-    def o_wait(count, j, arrival):
-        arrived(obuf.at[t_at(n_t - j), pl.ds(0, count * o_sub)], arrival)
+    def o_wait(count, p, arrival):
+        j, _, split = o_parts[p]
+        arrived(obuf.at[t_at(n_t - j), pl.ds(0, count * o_sub // split)], arrival)
 
     def w_spread(j):
         w_wait(1, j, w_first[j])
@@ -384,21 +394,20 @@
         w_wait(2, j, w_hops[j][1])
         settle(w_at, j, w_hops[j])
 
-    def o_spread(j):
-        o_wait(1, j, o_first[j])
-        spread(o_at, j, o_hops[j])
-
-    def o_relay(j):
-        o_wait(1, j, o_hops[j][0])
-        relay(o_at, j, o_hops[j])
-
-    def o_settle(j):
-        o_wait(2, j, o_hops[j][1])
-        settle(o_at, j, o_hops[j])
+    def o_spread(p):
+        o_wait(1, p, o_first[p])
+        spread(o_piece(p), o_parts[p][0], o_hops[p])
+
+    def o_relay(p):
+        o_wait(1, p, o_hops[p][0])
+        relay(o_piece(p), o_parts[p][0], o_hops[p])
+
+    def o_settle(p):
+        o_wait(2, p, o_hops[p][1])
+        settle(o_piece(p), o_parts[p][0], o_hops[p])
 
     one, three, two = others
-    o_early, o_late = (one, three), (two,)
-    o_a, o_b, o_c = o_early + o_late
+    o_a, o_b, o_c, o_d = range(n_t)
     k_wait(n_t - 1, k_first)
     for j in others:
         spread(k_at, j, k_hops)
@@ -407,7 +416,7 @@
     send_w(three)
     send_w(two)
     w_spread(one)
-    send_o(one)
+    send_o(o_a)
     k_wait(n_t - 1, k_hops[0])
     for j in others:
         relay(k_at, j, k_hops)
@@ -420,11 +429,11 @@
         packed[:, at] = x.astype(jnp.bfloat16)
         scaled[:, at] = (x * gain[:, at]).astype(jnp.bfloat16)
         squares += jnp.sum(x * x, axis=1, keepdims=True)
-    sq_part[...] = jnp.broadcast_to(pick(diagonal, squares, 0), (8, length))
+    sq_part[...] = pick(diagonal, squares, 0)
     sq_group = slot()
     for k in others:
         send(sq_part, sq_recv.at[k - 1], (me, t_at(k)), sq_group)
-    send_o(three)
+    send_o(o_b)
     w_spread(two)
     w_relay(one)
     k_wait(2 * (n_t - 1), k_hops[1])
@@ -433,12 +442,9 @@
     own_k.wait()
     k_wait(chips * (n_t - 1), k_hops[2])
     kv_groups = [slot() for _ in range(2)]
-    for c in range(2):
+
+    def send_kv(c):
         cols = slice(c * HD, (c + 1) * HD)
-        kv_part[:, cols] = lax.dot_general(
-            scaled[...], kbuf[cols, :], (((1,), (1,)), ((), ())),
-            preferred_element_type=jnp.float32,
-        ).astype(jnp.bfloat16)
         for k in others:
             to = t_at(k)
             send(
@@ -447,13 +453,22 @@
                 (me, to),
                 kv_groups[c],
             )
+
+    for c in range(2):
+        cols = slice(c * HD, (c + 1) * HD)
+        kv_part[:, cols] = lax.dot_general(
+            scaled[...], kbuf[cols, :], (((1,), (1,)), ((), ())),
+            preferred_element_type=jnp.float32,
+        ).astype(jnp.bfloat16)
         if c == 0:
-            send_o(two)
+            send_kv(0)
+            send_o(o_c)
+            send_o(o_d)
     w_relay(three)
     arrived(sq_recv, sq_group)
-    sq = sq_part[:1, :]
+    sq = sq_part[...]
     for k in range(n_t - 1):
-        sq += sq_recv[k, :1, :]
+        sq += sq_recv[k]
     inverse = lax.rsqrt(sq / (feat * n_t) + epsilon)
     inv_buf[...] = jnp.broadcast_to(pick(diagonal, inverse, 1), (length, HD))
 
@@ -490,21 +505,23 @@
             send(at, at, (me, t_at(k)), all_groups[c])
 
     w_relay(two)
+    o_spread(o_a)
     w_settle(one)
     share_kv(0)
+    send_kv(1)
     w_settle(three)
-    o_spread(o_a)
+    o_spread(o_b)
     w_wait(chips, one, w_hops[one][2])
     project(t_at(n_t - one))
     w_settle(two)
-    o_spread(o_b)
     w_wait(chips, three, w_hops[three][2])
     project(t_at(n_t - three))
+    o_relay(o_a)
+    o_spread(o_c)
     w_wait(chips, two, w_hops[two][2])
     project(t_at(n_t - two))
-    share_kv(1)
-    o_relay(o_a)
-    o_spread(o_c)
+    o_relay(o_b)
+    o_spread(o_d)
     arrived(kv_all.at[pl.ds(0, (n_t - 1) * rows), pl.ds(0, HD)], all_groups[0])
     lane = lax.broadcasted_iota(jnp.int32, (half, HD), 1)
     line = lax.broadcasted_iota(jnp.int32, (half, HD), 0)
@@ -524,11 +541,13 @@
     for k in others:
         send(score_part, score_recv.at[k - 1], (me, t_at(k)), score_group)
 
-    o_relay(o_b)
+    o_relay(o_c)
+    share_kv(1)
     o_settle(o_a)
-    o_relay(o_c)
+    o_relay(o_d)
     o_settle(o_b)
     o_settle(o_c)
+
     arrived(score_recv, score_group)
     total = score_part[...].astype(jnp.float32)
     for k in range(n_t - 1):
@@ -563,19 +582,30 @@
             dense, kv_all[:, HD:], preferred_element_type=jnp.float32
         ).astype(jnp.bfloat16)
 
+    o_settle(o_d)
     own_o.wait()
-    for j in others:
-        o_wait(chips, j, o_hops[j][2])
+    for p in (o_a, o_b):
+        o_wait(chips, p, o_hops[p][2])
+
+    last = t_at(n_t - two)
+
+    def take(u, at):
+        return jnp.dot(
+            ctx[:, pl.ds(aligned(u, o_rows), o_rows)], obuf[u, :, at],
+            preferred_element_type=jnp.float32,
+        )
 
     for i in range(tiles):
         at = slice(i * tile, (i + 1) * tile)
         result = packed[:, at].astype(jnp.float32)
-        for u in range(n_t):
-            result += jnp.dot(
-                ctx[:, u * o_rows : (u + 1) * o_rows],
-                obuf[u, :, at],
-                preferred_element_type=jnp.float32,
-            )
+        for u in (t, t_at(n_t - one), t_at(n_t - three)):
+            result += take(u, at)
+        acc[:, at] = result
+    for p in (o_c, o_d):
+        o_wait(chips, p, o_hops[p][2])
+    for i in range(tiles):
+        at = slice(i * tile, (i + 1) * tile)
+        result = acc[:, at] + take(last, at)
         out[:, at] = jnp.where(valid_buf[:, :1] > 0.0, result, 0.0).astype(jnp.bfloat16)
     for copy in started:
         copy.wait_send()
@@ -592,7 +622,7 @@
     cos_tab = np.concatenate([np.cos(angles)] * 2, axis=1).astype(np.float32)
     sin_tab = np.concatenate([-np.sin(angles), np.sin(angles)], axis=1).astype(np.float32)
     rows = length // n_t
-    groups = 4 + 8 * (n_t - 1) + 7
+    groups = 4 + 4 * (n_t - 1) + 4 * n_t + 7
     vmem = pl.BlockSpec(memory_space=pltpu.VMEM)
     hbm = pl.BlockSpec(memory_space=pltpu.HBM)
     bf, f32 = jnp.bfloat16, jnp.float32
@@ -626,10 +656,11 @@
             pltpu.VMEM((length, HD), f32),
             pltpu.VMEM((length, length), f32),
             pltpu.VMEM((length, HD), bf),
-            pltpu.VMEM((8, length), f32),
-            pltpu.VMEM((n_t - 1, 8, length), f32),
+            pltpu.VMEM((1, length), f32),
+            pltpu.VMEM((n_t - 1, 1, length), f32),
             pltpu.VMEM((length // 2, HD), bf),
             pltpu.VMEM((n_t - 1, length // 2, HD), bf),
+            pltpu.VMEM((length, feat), f32),
             pltpu.SemaphoreType.DMA,
             pltpu.SemaphoreType.DMA((groups,)),
             pltpu.SemaphoreType.DMA((8,)),

time: 44.1 us -> 42.8 us (0.971)
  Pallas kernels: 43.1 us -> 41.7 us
    pallas_call x1, Pallas kernels: 43.1 us -> 41.7 us  [fused_body(): pl.pallas_call(functools.partial(fused_kernel, (n_dp, n_t, length, feat,...]
where the time goes in v4:
time: 42.8 us; the launch traced here: 42.6 us
  Pallas kernels  41.7 us (97%)
  local copies, waits for them, and re-layouts  0.88 us (2%)
    pallas_call x1, Pallas kernels, fused_body(): pl.pallas_call(functools.partial(fused_kernel, (n_dp, n_t, length, feat,...  41.7 us
    unnamed x1, local copies, waits for them, and re-layouts  0.88 us

profile of v4, /device:TPU:0, one launch (start us, length us, event | category | flops | bytes accessed | tf_op | source)
XLA Modules:
  0.0 42.6 jit_solution(18127830118561586442)
XLA Ops:
  0.0 41.7 %shard_map.82 = bf16[256,1536]{1,0:T(8,128)(2,1)S(1)} custom-call(s32[1,256]{1,0:T(1,128)} %bitcast.5, s32[8,32]{1,0:T(8,128)} %len_hbm.1, f32[1,6144]{1,0:T(1,128)} %bitcast.4, f32[16,128]{1,0:T(8,128)} %constant.2.clone.tab_hbm, bf16[256,1536]{1,0:T(8,128)(2,1)} %roll_hbm.1, bf16[6144,256]{1,0:T(8,128)(2,1)} %w_in.1, bf16[64,6144]{1,0:T(8,128)(2,1)} %bitcast.3, ...), custom_call_target="tpu_custom_call" | custom-call | tf_op jit(solution)/shard_map/pallas_call | solution.py:629
  41.7 0.9 %copy.10 = bf16[256,1536]{1,0:T(8,128)(2,1)} copy(bf16[256,1536]{1,0:T(8,128)(2,1)S(1)} %shard_map.82) | data formatting | bytes 1572864

commit v5 on v4

--- a/solution.py
+++ b/solution.py
@@ -296,6 +296,7 @@
         )
 
     send_w(1)
+    send_w(others[1])
 
     o_parts = ((others[0], 0, 1), (others[1], 0, 1), (others[2], 0, 2), (others[2], 1, 2))
 
@@ -413,7 +414,6 @@
         spread(k_at, j, k_hops)
     for c in range(CORES):
         send_rows(other_chip * CORES + lax.rem(core + c, CORES))
-    send_w(three)
     send_w(two)
     w_spread(one)
     send_o(o_a)

time: 42.8 us -> 42.8 us (level)
  no operation moved by 1% of the time
where the time goes in v5:
time: 42.8 us; the launch traced here: 42.6 us
  Pallas kernels  41.7 us (97%)
  local copies, waits for them, and re-layouts  0.88 us (2%)
    pallas_call x1, Pallas kernels, fused_body(): pl.pallas_call(functools.partial(fused_kernel, (n_dp, n_t, length, feat,...  41.7 us
    unnamed x1, local copies, waits for them, and re-layouts  0.88 us

profile of v5, /device:TPU:0, one launch (start us, length us, event | category | flops | bytes accessed | tf_op | source)
XLA Modules:
  0.0 42.6 jit_solution(330443102692399697)
XLA Ops:
  0.0 41.7 %shard_map.82 = bf16[256,1536]{1,0:T(8,128)(2,1)S(1)} custom-call(s32[1,256]{1,0:T(1,128)} %bitcast.5, s32[8,32]{1,0:T(8,128)} %len_hbm.1, f32[1,6144]{1,0:T(1,128)} %bitcast.4, f32[16,128]{1,0:T(8,128)} %constant.2.clone.tab_hbm, bf16[256,1536]{1,0:T(8,128)(2,1)} %roll_hbm.1, bf16[6144,256]{1,0:T(8,128)(2,1)} %w_in.1, bf16[64,6144]{1,0:T(8,128)(2,1)} %bitcast.3, ...), custom_call_target="tpu_custom_call" | custom-call | tf_op jit(solution)/shard_map/pallas_call | solution.py:629
  41.7 0.9 %copy.10 = bf16[256,1536]{1,0:T(8,128)(2,1)} copy(bf16[256,1536]{1,0:T(8,128)(2,1)S(1)} %shard_map.82) | data formatting | bytes 1572864
